TPU v7x, 32 devices: a whole 2x2x4 slice. The times are simulated.
32 devices in a mesh: row: 8 (over z, y), col: 4 (over x, core).
Axes of the slice: x: 2, y: 2, z: 4, core: 2. Of those that a mesh axis runs over, the one named last changes fastest.
Arguments:
- tracer: float32 [128, 128, 512], P(None, 'row', 'col'), may hold values from -6 to 6
- symbol_x: float32 [128], replicated, may hold values from 0.3 to 3
- symbol_y: float32 [128], replicated, may hold values from 0.3 to 3
- symbol_z: float32 [512], replicated, may hold values from 0.3 to 3
Outputs:
- spectrum: float32 [128, 128, 512], P('row', 'col')
All inputs are finite; a program needn't handle non-finite values.
Results may differ from a plain program's by a relative error of at most 0.000075.
Values sent between devices are 32-bit elements; how exact they have to be, the bound alone decides.
A program may use at most 64 MiB of HBM per device.

v0:
```python
import jax
import jax.numpy as jnp
from jax import lax
from jax.sharding import PartitionSpec as P


def transform_table(count):
    rank = jnp.arange(count)
    angle = (
        jnp.pi
        / (count + 1)
        * ((rank[:, None] + 1) * (rank[None, :] + 1) % (2 * count + 2)).astype(jnp.float32)
    )
    return jnp.sin(angle) * (2.0 / (count + 1)) ** 0.5


def to_modes(values, dim):
    moved = jnp.tensordot(
        values,
        transform_table(values.shape[dim]),
        axes=([dim], [0]),
        precision=lax.Precision.HIGHEST,
    )
    return jnp.moveaxis(moved, -1, dim)


def per_device(tracer, symbol_x, symbol_y, symbol_z):
    part_values = tracer
    part_values = to_modes(part_values, 0)
    part_values = lax.all_to_all(part_values, "row", split_axis=0, concat_axis=1, tiled=True)
    part_values = to_modes(part_values, 1)
    local_values = part_values
    local_values = lax.all_to_all(local_values, "col", split_axis=1, concat_axis=2, tiled=True)
    local_values = to_modes(local_values, 2)
    share_x = local_values.shape[0]
    part_x = lax.dynamic_slice_in_dim(symbol_x, lax.axis_index("row") * share_x, share_x)
    share_y = local_values.shape[1]
    part_y = lax.dynamic_slice_in_dim(symbol_y, lax.axis_index("col") * share_y, share_y)
    symbol = part_x[:, None, None] + part_y[None, :, None] + symbol_z[None, None, :]
    local_values = local_values * ((1.0 - 0.2 * symbol) / (1.0 + 0.2 * symbol))
    return local_values


def solution(mesh):
    in_specs = (P(None, "row", "col"), P(), P(), P())
    out_specs = P("row", "col", None)
    return jax.shard_map(
        per_device, mesh=mesh, in_specs=in_specs, out_specs=out_specs, check_vma=False
    )
```

profile of v0, /device:TPU:0, one launch (start us, length us, event | category | flops | bytes accessed | tf_op | source)
XLA Modules:
  0.0 66.0 jit_solution(14999294112049493810)
XLA Ops:
  0.0 0.0 copy-start
  0.0 1.2 %copy-done = f32[128,16,128]{2,1,0:T(8,128)S(1)} copy-done((f32[128,16,128]{2,1,0:T(8,128)S(1)}, f32[128,16,128]{2,1,0:T(8,128)}, u32[]{:S(2)}) %copy-start) | copy-done | bytes 1048600
  1.2 1.6 %fusion.6 = f32[128,16,128]{2,0,1:T(8,128)S(1)} fusion(f32[128,16,128]{2,1,0:T(8,128)S(1)} %copy-done, s32[128]{0:T(128)S(1)} %iota_add_fusion.1), kind=kOutput, calls=%fused_computation.8 | convolution fusion | flops 402817024 | bytes 2097664 | tf_op jit(solution)/shard_map/dot_general | solution.py:18
  2.8 0.6 copy.24
  3.5 32.9 %all_to_all.36 = f32[128,16,128]{2,1,0:T(8,128)S(1)} all-to-all(f32[128,16,128]{2,1,0:T(8,128)S(1)} %copy.24), channel_id=1, replica_groups=mesh['row'=8,'col'=4] {'row'}, dimensions={0} | all-to-all | bytes 2097152 | tf_op jit(solution)/shard_map/all_to_all | solution.py:30
  36.3 0.1 copy.25
  36.4 2.0 %convolution_bitcast_fusion = f32[16,128,128]{1,2,0:T(8,128)S(1)} fusion(f32[16,128,128]{2,1,0:T(8,128)S(1)} %bitcast.21, s32[128]{0:T(128)S(1)} %iota_add_fusion.1), kind=kOutput, calls=%fused_computation.2 | convolution fusion | flops 402817024 | bytes 2097664 | tf_op jit(solution)/shard_map/dot_general | solution.py:18
  38.4 1.4 %copy.27 = f32[16,128,128]{2,0,1:T(8,128)} copy(f32[16,128,128]{1,2,0:T(8,128)S(1)} %convolution_bitcast_fusion) | data formatting | bytes 2097152 | tf_op jit(solution)/shard_map/transpose | solution.py:24
  39.8 3.7 %all-to-all-start.1 = ((f32[16,128,128]{2,0,1:T(8,128)}), f32[16,128,128]{2,0,1:T(8,128)S(1)}, u32[]{:S(2)}, u32[]{:S(2)}) async-start(f32[16,128,128]{2,0,1:T(8,128)} %copy.27), calls=%async_computation.1 | async-start | bytes 2097152 | tf_op jit(solution)/shard_map/all_to_all | solution.py:33
  43.5 0.0 copy-start.2
  43.5 0.6 copy-done.2
  44.2 0.1 dynamic_slice.7
  44.2 0.0 copy-start.3
  44.2 0.7 copy-done.3
  44.9 0.1 dynamic_slice.6
  45.0 0.1 broadcast_add_fusion
  45.0 12.7 %all-to-all-done.1 = f32[16,128,128]{2,0,1:T(8,128)S(1)} async-done(((f32[16,128,128]{2,0,1:T(8,128)}), f32[16,128,128]{2,0,1:T(8,128)S(1)}, u32[]{:S(2)}, u32[]{:S(2)}) %all-to-all-start.1) | async-done | bytes 1048608 | tf_op jit(solution)/shard_map/all_to_all | solution.py:33
  57.7 0.7 %copy.29 = f32[16,32,4,128]{3,2,1,0:T(4,128)S(1)} copy(f32[16,32,4,128]{3,0,1,2:T(8,128)S(1)} %bitcast.19) | data formatting | bytes 2097152 | tf_op jit(solution)/shard_map/all_to_all | solution.py:33
  58.4 0.0 copy-start.1
  58.4 0.4 all_to_all.33
  58.8 0.2 copy-done.1
  59.1 7.0 %convolution_multiply_fusion = f32[16,32,512]{2,1,0:T(8,128)} fusion(f32[16,32,512]{2,1,0:T(8,128)S(1)} %all_to_all.33, f32[512]{0:T(512)S(1)} %copy-done.1, f32[16,32]{1,0:T(8,128)S(1)} %broadcast_add_fusion, s32[512]{0:T(512)S(1)} %iota_add_fusion), kind=kOutput, calls=%fused_computation.1 | convolution fusion | flops 1614807040 | bytes 2103296 | tf_op jit(solution)/shard_map/dot_general | solution.py:18
  (2 shorter events, 0.0 us)
Async XLA Ops:
  0.0 1.2 %copy-start = (f32[128,16,128]{2,1,0:T(8,128)S(1)}, f32[128,16,128]{2,1,0:T(8,128)}, u32[]{:S(2)}) copy-start(f32[128,16,128]{2,1,0:T(8,128)} %param.4) | copy-start | bytes 3145732
  39.8 17.9 %all-to-all-start.1 = ((f32[16,128,128]{2,0,1:T(8,128)}), f32[16,128,128]{2,0,1:T(8,128)S(1)}, u32[]{:S(2)}, u32[]{:S(2)}) async-start(f32[16,128,128]{2,0,1:T(8,128)} %copy.27), calls=%async_computation.1 | async-start | bytes 2097152 | tf_op jit(solution)/shard_map/all_to_all | solution.py:33
  43.5 0.7 copy-start.2
  44.2 0.7 copy-start.3
  58.4 0.7 %copy-start.1 = (f32[512]{0:T(512)S(1)}, f32[512]{0:T(512)}, u32[]{:S(2)}) copy-start(f32[512]{0:T(512)} %param.7) | copy-start | bytes 6148
where the time goes:
time: 66.3 us; the launch traced here: 66 us
  blocking collectives  32.9 us (50%)
  waiting for transfers between devices  12.7 us (19%)
  matrix products  10.5 us (16%)
  local copies, waits for them, and re-layouts  6.11 us (9%)
  starting transfers between devices  3.7 us (6%)
    all_to_all x1, blocking collectives, per_device(): lax.all_to_all(part_values, 'row', split_axis=0, concat_axis=1, tiled=True)  32.9 us
    all_to_all x1, waiting for transfers between devices, per_device(): lax.all_to_all(local_values, 'col', split_axis=1, concat_axis=2, tiled=True)  12.7 us
    dot_general x3, matrix products, to_modes(): jnp.tensordot(values, transform_table(values.shape[dim]), axes=([dim], [0...  10.5 us
    all_to_all x1, starting transfers between devices, per_device(): lax.all_to_all(local_values, 'col', split_axis=1, concat_axis=2, tiled=True)  3.7 us
    unnamed x8, local copies, waits for them, and re-layouts  2.77 us
    transpose x1, local copies, waits for them, and re-layouts, to_modes(): return jnp.moveaxis(moved, -1, dim)  1.38 us
  transfers between devices with their start and end apart: 1, of which 1 were waited for; matrix products, arithmetic and copies ran while one was open for 0% of the time, Pallas kernels for 0%

commit v1 on v0

v1 whole, which is shorter than its diff:
```python
import functools

import jax
import jax.numpy as jnp
import ml_dtypes
import numpy as np
from jax import lax
from jax.experimental import pallas as pl
from jax.experimental.pallas import tpu as pltpu
from jax.sharding import PartitionSpec as P

MESH = pl.DeviceIdType.MESH
F32 = jnp.float32
BF16 = jnp.bfloat16
PIECES = 8


def table_halves(count):
    rank = np.arange(1, count + 1)
    turns = np.outer(rank, rank) % (2 * count + 2)
    table = np.sin(np.pi / (count + 1) * turns) * np.sqrt(2.0 / (count + 1))
    high = table.astype(ml_dtypes.bfloat16)
    low = (table - high.astype(np.float64)).astype(ml_dtypes.bfloat16)
    return high, low


def halves(values):
    high = values.astype(BF16)
    return high, (values - high.astype(F32)).astype(BF16)


def dot(a, b):
    return jnp.dot(a, b, preferred_element_type=F32)


def from_left(stacked, values):
    rows = stacked.shape[0] // 2
    high, low = halves(values)
    both = dot(stacked, high)
    return both[:rows] + both[rows:] + dot(stacked[:rows], low)


def kernel(
    n, m, pieces, groups, block,
    field, tab_x, tab_y, tab_zh, tab_zl, sx, sy, sz, out,
    d, s, r, y, c, f, o, tx, ty, tzh, tzl, colx, coly, vx, vy, vz,
    in_sem, tab_sem, send_r, recv_r, send_c, recv_c, out_sem,
):
    me_r, me_c = lax.axis_index("row"), lax.axis_index("col")
    depth, ys, zs = d.shape
    each = r.shape[0] // pieces
    per = n * each
    yc = y.shape[3]
    loads = [(field, d, 0), (tab_x, tx, 1), (tab_y, ty, 2), (tab_zh, tzh, 3), (tab_zl, tzl, 4)]
    loads += [(sx, vx, 5), (sy, vy, 6), (sz, vz, 7)]
    loads = [pltpu.make_async_copy(a, b, in_sem.at[i]) for a, b, i in loads]
    for load in loads:
        load.start()

    barrier = pltpu.get_barrier_semaphore()

    def greet(axis, me, size):
        def one(i, _):
            pl.semaphore_signal(
                barrier, inc=1, device_id={axis: lax.rem(me + i, size)}, device_id_type=MESH
            )
            return 0

        lax.fori_loop(1, size, one, 0)

    greet("row", me_r, n)
    greet("col", me_c, m)

    loads[0].wait()
    loads[1].wait()
    lanes = d.reshape(depth * ys, zs)
    modes = s.reshape(s.shape[0] * ys, zs)

    def transform_x(first, count):
        rows = count * per
        stacked = tx[2 * first * per : 2 * (first + count) * per]

        def pair(i, _):
            got = jnp.concatenate(
                [lanes[pl.ds(2 * i + h, depth, stride=ys), :] for h in range(2)], axis=1
            )
            got = from_left(stacked, got)
            for h in range(2):
                modes[pl.ds(first * per * ys + 2 * i + h, rows, stride=ys), :] = got[
                    :, h * zs : (h + 1) * zs
                ]
            return 0

        lax.fori_loop(0, ys // 2, pair, 0, unroll=True)

    def send_rows(k):
        def one(i, _):
            step = n // 2 + (i + 1) // 2 * (2 * (i % 2) - 1)
            to = lax.rem(me_r + step, n)
            pltpu.make_async_remote_copy(
                src_ref=s.at[pl.ds(k * per + to * each, each)],
                dst_ref=r.at[pl.ds(k * each, each), pl.ds(pl.multiple_of(me_r * ys, ys), ys), :],
                send_sem=send_r.at[k],
                recv_sem=recv_r.at[k],
                device_id={"row": to},
                device_id_type=MESH,
            ).start()
            return 0

        lax.fori_loop(0, n - 1, one, 0)
        r[pl.ds(k * each, each), pl.ds(pl.multiple_of(me_r * ys, ys), ys), :] = s[
            pl.ds(k * per + me_r * each, each)
        ]

    for at, (first, count) in enumerate(groups):
        transform_x(first, count)
        if at == 0:
            pl.semaphore_wait(barrier, n + m - 2)
        for k in range(first, first + count):
            send_rows(k)

    for load in loads[2:]:
        load.wait()

    def upright(row_ref, into):
        size = row_ref.shape[1]
        here = lax.broadcasted_iota(jnp.int32, (size, size), 0)
        there = lax.broadcasted_iota(jnp.int32, (size, size), 1)
        kept = jnp.where(here == there, row_ref[...], 0.0)
        into[...] = jnp.broadcast_to(jnp.sum(kept, axis=1, keepdims=True), into.shape)

    upright(vx, colx)
    upright(vy, coly)
    x_share = r.shape[0]
    part_y = coly[pl.ds(pl.multiple_of(me_c * yc, yc), yc), :]

    def factor(i, _):
        symbol = part_y + colx[pl.ds(me_r * x_share + i, 1), :]
        for at in range(0, vz.shape[1], 128):
            full = symbol + vz[:, at : at + 128]
            f[pl.ds(pl.multiple_of(i * yc, yc), yc), at : at + 128] = (1.0 - 0.2 * full) / (
                1.0 + 0.2 * full
            )
        return 0

    lax.fori_loop(0, x_share, factor, 0)

    def got_rows(k):
        waited = r.at[pl.ds(k * each, each), pl.ds(0, (n - 1) * ys), :]
        pltpu.make_async_copy(waited, waited, recv_r.at[k]).wait()

    def transform_y(k):
        got = jnp.concatenate([r[k * each + j] for j in range(each)], axis=1)
        for b in range(ty.shape[0] // (2 * block)):
            now = from_left(ty[2 * b * block : 2 * (b + 1) * block], got)
            for q in range(block // yc):
                for j in range(each):
                    y[k, b * (block // yc) + q, j] = now[
                        q * yc : (q + 1) * yc, j * zs : (j + 1) * zs
                    ]

    def send_cols(k):
        def one(i, _):
            to = lax.rem(me_c + i, m)
            pltpu.make_async_remote_copy(
                src_ref=y.at[k, to],
                dst_ref=c.at[k, me_c],
                send_sem=send_c.at[k],
                recv_sem=recv_c.at[k],
                device_id={"col": to},
                device_id_type=MESH,
            ).start()
            return 0

        lax.fori_loop(1, m, one, 0)
        c[k, me_c] = y[k, me_c]

    def got_cols(k):
        waited = c.at[k, pl.ds(0, m - 1)]
        pltpu.make_async_copy(waited, waited, recv_c.at[k]).wait()

    def written(k):
        rows = pl.ds(pl.multiple_of(k * each * yc, each * yc), each * yc)
        return pltpu.make_async_copy(o.at[rows, :], out.at[rows, :], out_sem.at[k])

    def transform_z(k):
        rows = each * yc
        got = jnp.concatenate([c[k, q].reshape(rows, zs) for q in range(m)], axis=1)
        high, low = halves(got)
        both = dot(jnp.concatenate([high, low], axis=0), tzh[...])
        full = both[:rows] + both[rows:] + dot(high, tzl[...])
        at = pl.ds(pl.multiple_of(k * rows, rows), rows)
        o[at, :] = full * f[at, :]
        written(k).start()

    def step(k, _):
        got_rows(k)
        transform_y(k)
        send_cols(k)

        @pl.when(k > 0)
        def _():
            got_cols(k - 1)
            transform_z(k - 1)

        return 0

    lax.fori_loop(0, pieces, step, 0)
    got_cols(pieces - 1)
    transform_z(pieces - 1)

    def finish(k, _):
        sent = s.at[pl.ds(0, (n - 1) * each)]
        pltpu.make_async_copy(sent, sent, send_r.at[k]).wait()
        sent = y.at[k, pl.ds(0, m - 1)]
        pltpu.make_async_copy(sent, sent, send_c.at[k]).wait()
        written(k).wait()
        return 0

    lax.fori_loop(0, pieces, finish, 0)


def per_device(n, m, tracer, symbol_x, symbol_y, symbol_z):
    depth, ys, zs = tracer.shape
    height, length = ys * n, zs * m
    x_share, yc = depth // n, height // m
    pieces = min(PIECES, x_share)
    each = x_share // pieces
    per = n * each
    block = min(height, 128)

    groups = [(0, 1)]
    most = max(1, 128 // per)
    while sum(groups[-1]) < pieces:
        first = sum(groups[-1])
        groups.append((first, min(most, pieces - first)))
    order = np.arange(depth).reshape(n, pieces, each).transpose(1, 0, 2).reshape(pieces, per)
    high, low = table_halves(depth)
    tab_x = []
    for first, count in groups:
        rows = order[first : first + count].reshape(-1)
        tab_x += [high[rows], low[rows]]
    tab_x = np.concatenate(tab_x)
    high, low = table_halves(height)
    tab_y = []
    for b in range(0, height, block):
        tab_y += [high[b : b + block], low[b : b + block]]
    tab_y = np.concatenate(tab_y)
    tab_zh, tab_zl = table_halves(length)

    anywhere = pl.BlockSpec(memory_space=pl.ANY)
    dma = pltpu.SemaphoreType.DMA
    out = pl.pallas_call(
        functools.partial(kernel, n, m, pieces, groups, block),
        out_shape=jax.ShapeDtypeStruct((x_share * yc, length), F32),
        in_specs=[anywhere] * 8,
        out_specs=anywhere,
        scratch_shapes=[
            pltpu.VMEM((depth, ys, zs), F32),
            pltpu.VMEM((depth, ys, zs), F32),
            pltpu.VMEM((x_share, height, zs), F32),
            pltpu.VMEM((pieces, m, each, yc, zs), F32),
            pltpu.VMEM((pieces, m, each, yc, zs), F32),
            pltpu.VMEM((x_share * yc, length), F32),
            pltpu.VMEM((x_share * yc, length), F32),
            pltpu.VMEM(tab_x.shape, BF16),
            pltpu.VMEM(tab_y.shape, BF16),
            pltpu.VMEM(tab_zh.shape, BF16),
            pltpu.VMEM(tab_zl.shape, BF16),
            pltpu.VMEM((depth, 128), F32),
            pltpu.VMEM((height, 128), F32),
            pltpu.VMEM((1, depth), F32),
            pltpu.VMEM((1, height), F32),
            pltpu.VMEM((1, length), F32),
            dma((8,)),
            dma((1,)),
            dma((pieces,)),
            dma((pieces,)),
            dma((pieces,)),
            dma((pieces,)),
            dma((pieces,)),
        ],
        compiler_params=pltpu.CompilerParams(collective_id=0, has_side_effects=True),
    )(
        tracer,
        jnp.asarray(tab_x),
        jnp.asarray(tab_y),
        jnp.asarray(tab_zh),
        jnp.asarray(tab_zl),
        symbol_x[None],
        symbol_y[None],
        symbol_z[None],
    )
    return out.reshape(x_share, yc, length)


def solution(mesh):
    in_specs = (P(None, "row", "col"), P(), P(), P())
    out_specs = P("row", "col", None)
    body = functools.partial(per_device, mesh.shape["row"], mesh.shape["col"])
    return jax.shard_map(
        body, mesh=mesh, in_specs=in_specs, out_specs=out_specs, check_vma=False
    )
```

time: 66.3 us -> 38.3 us (0.58)
  Pallas kernels: 0 us -> 35.9 us
  blocking collectives: 32.9 us -> 0 us
  waiting for transfers between devices: 12.7 us -> 0 us
  matrix products: 10.5 us -> 0 us
  local copies, waits for them, and re-layouts: 6.11 us -> 2.29 us
  starting transfers between devices: 3.7 us -> 0 us
    pallas_call x0 -> x1, Pallas kernels: none -> 35.9 us  [per_device(): pl.pallas_call(functools.partial(kernel, n, m, pieces, groups, block), ou...]
    all_to_all x1 -> x0, blocking collectives: 32.9 us -> none  [per_device(): lax.all_to_all(part_values, 'row', split_axis=0, concat_axis=1, tiled=True)]
    all_to_all x1 -> x0, waiting for transfers between devices: 12.7 us -> none  [per_device(): lax.all_to_all(local_values, 'col', split_axis=1, concat_axis=2, tiled=True)]
    dot_general x3 -> x0, matrix products: 10.5 us -> none  [to_modes(): jnp.tensordot(values, transform_table(values.shape[dim]), axes=([dim], [0...]
    all_to_all x1 -> x0, starting transfers between devices: 3.7 us -> none  [per_device(): lax.all_to_all(local_values, 'col', split_axis=1, concat_axis=2, tiled=True)]
    transpose x1 -> x0, local copies, waits for them, and re-layouts: 1.38 us -> none  [to_modes(): return jnp.moveaxis(moved, -1, dim)]
    all_to_all x3 -> x0, local copies, waits for them, and re-layouts: 1.2 us -> none  [the longest x2 1.1 us: per_device(): lax.all_to_all(local_values, 'col', split_axis=1, concat_axis=2, tiled=True)]
    unnamed x8 -> x1, local copies, waits for them, and re-layouts: 2.77 us -> 2.29 us
  transfers between devices with their start and end apart: 1 -> 0, of which waited for: 1 -> 0; matrix products, arithmetic and copies ran while one was open for 0% -> 0% of each run, Pallas kernels for 0% -> 0%
where the time goes in v1:
time: 38.3 us; the launch traced here: 38.2 us
  Pallas kernels  35.9 us (94%)
  local copies, waits for them, and re-layouts  2.29 us (6%)
    pallas_call x1, Pallas kernels, per_device(): pl.pallas_call(functools.partial(kernel, n, m, pieces, groups, block), ou...  35.9 us
    unnamed x1, local copies, waits for them, and re-layouts  2.29 us

profile of v1, /device:TPU:0, one launch (start us, length us, event | category | flops | bytes accessed | tf_op | source)
XLA Modules:
  0.0 38.2 jit_solution(15894640951598231611)
XLA Ops:
  0.0 35.9 %shard_map.82 = f32[512,512]{1,0:T(8,128)} custom-call(f32[128,16,128]{2,1,0:T(8,128)} %field.1, bf16[256,128]{1,0:T(8,128)(2,1)} %constant.8.clone.tab_x, bf16[256,128]{1,0:T(8,128)(2,1)} %constant.9.clone.tab_y, bf16[512,512]{1,0:T(8,128)(2,1)} %constant.10.clone.tab_zh, bf16[512,512]{1,0:T(8,128)(2,1)} %constant.11.clone.tab_zl, f32[1,128]{1,0:T(1,128)} %bitcast.6, ...), custom_call_target="tpu_custom_call" | custom-call | tf_op jit(solution)/shard_map/pallas_call | solution.py:253
  35.9 2.3 %copy.10 = f32[16,32,512]{2,1,0:T(8,128)} copy(f32[16,32,512]{2,1,0:T(8,128)} %bitcast.4) | data formatting | bytes 2097152

commit v2 on v1

--- a/solution.py
+++ b/solution.py
@@ -12,7 +12,8 @@
 MESH = pl.DeviceIdType.MESH
 F32 = jnp.float32
 BF16 = jnp.bfloat16
-PIECES = 8
+PIECES = 4
+LAG = 1
 
 
 def table_halves(count):
@@ -43,9 +44,10 @@
 def kernel(
     n, m, pieces, groups, block,
     field, tab_x, tab_y, tab_zh, tab_zl, sx, sy, sz, out,
-    d, s, r, y, c, f, o, tx, ty, tzh, tzl, colx, coly, vx, vy, vz,
-    in_sem, tab_sem, send_r, recv_r, send_c, recv_c, out_sem,
+    d, s, r, y, c, f, tx, ty, tzh, tzl, colx, coly, vx, vy, vz,
+    in_sem, tab_sem, send_r, recv_r, send_c, recv_c,
 ):
+    lag = min(LAG, pieces)
     me_r, me_c = lax.axis_index("row"), lax.axis_index("col")
     depth, ys, zs = d.shape
     each = r.shape[0] // pieces
@@ -95,8 +97,7 @@
 
     def send_rows(k):
         def one(i, _):
-            step = n // 2 + (i + 1) // 2 * (2 * (i % 2) - 1)
-            to = lax.rem(me_r + step, n)
+            to = lax.rem(me_r + 1 + i, n)
             pltpu.make_async_remote_copy(
                 src_ref=s.at[pl.ds(k * per + to * each, each)],
                 dst_ref=r.at[pl.ds(k * each, each), pl.ds(pl.multiple_of(me_r * ys, ys), ys), :],
@@ -179,10 +180,6 @@
         waited = c.at[k, pl.ds(0, m - 1)]
         pltpu.make_async_copy(waited, waited, recv_c.at[k]).wait()
 
-    def written(k):
-        rows = pl.ds(pl.multiple_of(k * each * yc, each * yc), each * yc)
-        return pltpu.make_async_copy(o.at[rows, :], out.at[rows, :], out_sem.at[k])
-
     def transform_z(k):
         rows = each * yc
         got = jnp.concatenate([c[k, q].reshape(rows, zs) for q in range(m)], axis=1)
@@ -190,31 +187,33 @@
         both = dot(jnp.concatenate([high, low], axis=0), tzh[...])
         full = both[:rows] + both[rows:] + dot(high, tzl[...])
         at = pl.ds(pl.multiple_of(k * rows, rows), rows)
-        o[at, :] = full * f[at, :]
-        written(k).start()
+        out[at, :] = full * f[at, :]
 
     def step(k, _):
         got_rows(k)
         transform_y(k)
         send_cols(k)
 
-        @pl.when(k > 0)
+        @pl.when(k >= lag)
         def _():
-            got_cols(k - 1)
-            transform_z(k - 1)
+            got_cols(k - lag)
+            transform_z(k - lag)
 
         return 0
 
     lax.fori_loop(0, pieces, step, 0)
-    got_cols(pieces - 1)
-    transform_z(pieces - 1)
+    def drain(k, _):
+        got_cols(k)
+        transform_z(k)
+        return 0
+
+    lax.fori_loop(pieces - lag, pieces, drain, 0)
 
     def finish(k, _):
         sent = s.at[pl.ds(0, (n - 1) * each)]
         pltpu.make_async_copy(sent, sent, send_r.at[k]).wait()
         sent = y.at[k, pl.ds(0, m - 1)]
         pltpu.make_async_copy(sent, sent, send_c.at[k]).wait()
-        written(k).wait()
         return 0
 
     lax.fori_loop(0, pieces, finish, 0)
@@ -252,16 +251,15 @@
     dma = pltpu.SemaphoreType.DMA
     out = pl.pallas_call(
         functools.partial(kernel, n, m, pieces, groups, block),
-        out_shape=jax.ShapeDtypeStruct((x_share * yc, length), F32),
+        out_shape=pltpu.VMEM((x_share * yc, length), F32),
         in_specs=[anywhere] * 8,
-        out_specs=anywhere,
+        out_specs=pl.BlockSpec(memory_space=pltpu.VMEM),
         scratch_shapes=[
             pltpu.VMEM((depth, ys, zs), F32),
             pltpu.VMEM((depth, ys, zs), F32),
             pltpu.VMEM((x_share, height, zs), F32),
             pltpu.VMEM((pieces, m, each, yc, zs), F32),
             pltpu.VMEM((pieces, m, each, yc, zs), F32),
-            pltpu.VMEM((x_share * yc, length), F32),
             pltpu.VMEM((x_share * yc, length), F32),
             pltpu.VMEM(tab_x.shape, BF16),
             pltpu.VMEM(tab_y.shape, BF16),
@@ -278,9 +276,12 @@
             dma((pieces,)),
             dma((pieces,)),
             dma((pieces,)),
-            dma((pieces,)),
         ],
-        compiler_params=pltpu.CompilerParams(collective_id=0, has_side_effects=True),
+        compiler_params=pltpu.CompilerParams(
+            collective_id=0,
+            has_side_effects=True,
+            vmem_limit_bytes=(58 << 20) - 12 * x_share * yc * length,
+        ),
     )(
         tracer,
         jnp.asarray(tab_x),

time: 38.3 us -> 34.5 us (0.901)
  Pallas kernels: 35.9 us -> 33.3 us
  local copies, waits for them, and re-layouts: 2.29 us -> 0.97 us
    pallas_call x1, Pallas kernels: 35.9 us -> 33.3 us  [per_device(): pl.pallas_call(functools.partial(kernel, n, m, pieces, groups, block), ou...]
    unnamed x1, local copies, waits for them, and re-layouts: 2.29 us -> 0.97 us
where the time goes in v2:
time: 34.5 us; the launch traced here: 34.3 us
  Pallas kernels  33.3 us (97%)
  local copies, waits for them, and re-layouts  0.97 us (3%)
    pallas_call x1, Pallas kernels, per_device(): pl.pallas_call(functools.partial(kernel, n, m, pieces, groups, block), ou...  33.3 us
    unnamed x1, local copies, waits for them, and re-layouts  0.97 us

profile of v2, /device:TPU:0, one launch (start us, length us, event | category | flops | bytes accessed | tf_op | source)
XLA Modules:
  0.0 34.3 jit_solution(5731421183728547542)
XLA Ops:
  0.0 33.3 %shard_map.82 = f32[512,512]{1,0:T(8,128)S(1)} custom-call(f32[128,16,128]{2,1,0:T(8,128)} %field.1, bf16[256,128]{1,0:T(8,128)(2,1)} %constant.8.clone.tab_x, bf16[256,128]{1,0:T(8,128)(2,1)} %constant.9.clone.tab_y, bf16[512,512]{1,0:T(8,128)(2,1)} %constant.10.clone.tab_zh, bf16[512,512]{1,0:T(8,128)(2,1)} %constant.11.clone.tab_zl, f32[1,128]{1,0:T(1,128)} %bitcast.6, ...), custom_call_target="tpu_custom_call" | custom-call | tf_op jit(solution)/shard_map/pallas_call | solution.py:252
  33.3 1.0 %copy.10 = f32[16,32,512]{2,1,0:T(8,128)} copy(f32[16,32,512]{2,1,0:T(8,128)S(1)} %bitcast.4) | data formatting | bytes 2097152
